TPU v7x, 32 devices: a whole 2x2x4 slice. The times are simulated.
32 devices in a mesh: panel: 16 (over z, y, x), lag: 2 (over core).
Axes of the slice: x: 2, y: 2, z: 4, core: 2. Of those that a mesh axis runs over, the one named last changes fastest.
Arguments:
- history: bfloat16 [2, 32, 512, 128], P('lag', 'panel'), may hold values from -6 to 6
- weights: bfloat16 [16, 2, 6, 512, 512], P('panel', 'lag'), may hold values from -0.25 to 0.25
- pairs: int32 [16, 2, 6, 3], P('panel', 'lag'), may hold values from 0 to 4, as said below
- counts: int32 [16, 2], P('panel', 'lag'), may hold values from 3 to 6, as said below
- send_list: int32 [16, 2, 5, 2], P(None, 'lag'), may hold values from 0 to 1
- incident: bfloat16 [32, 512, 128], P(('panel', 'lag')), may hold values from -6 to 6
- near_inverse: bfloat16 [32, 512, 512], P(('panel', 'lag')), may hold values from -0.25 to 0.25
Outputs:
- density: bfloat16 [32, 512, 128], P(('panel', 'lag'))
Inputs may be any that keep to these rules, and one draw needn't show every extreme that they name: pairs[p, g, k] = (o, c, r) with o in 0 to 4, c in 0 to 1, r in 0 to 1; the (o, c) of one device's pairs are distinct. `counts`: panel index 0 at lag index 0 has 6 pairs.
All inputs are finite; a program needn't handle non-finite values.
Results may differ from a plain program's by a relative error of at most 0.0083.
Values may be sent and summed in bfloat16 or wider, within the bound.
A program may use at most 64 MiB of HBM per device.

v0:
```python
import functools

import jax
import jax.numpy as jnp
from jax import lax
from jax.experimental import pallas as pl
from jax.experimental.pallas import tpu as pltpu
from jax.sharding import PartitionSpec as P

CHUNKS = 2


def step_kernel(
    relay, panels, lags,
    pairs_ref, counts_ref, send_ref, local_ref, weights_ref, incident_ref, near_ref,
    out_ref,
    window, weights, near, incident, right, partial_value, landed,
    send_sem, recv_sem, local_sem, weight_sem, near_sem, incident_sem,
    sum_send_sem, sum_recv_sem,
):
    here = lax.axis_index("panel")
    lag = lax.axis_index("lag")
    offsets = send_ref.shape[1]
    reach = offsets // 2
    blocks, depth, fields = window.shape[1:]
    count = weights.shape[0]
    own = incident.shape[0]
    side = 2 * lax.rem(here, 2) - 1

    def panel(steps):
        return lax.rem(here + steps + panels, panels)

    def outgoing(steps):
        return local_ref.at[reach - steps] if not relay else window.at[0]

    source_here = local_ref.at[0] if relay else local_ref.at[reach]
    local = pltpu.make_async_copy(source_here, window.at[0], local_sem)
    local.start()
    weight_copies = [
        pltpu.make_async_copy(weights_ref.at[0, 0, k], weights.at[k], weight_sem.at[k])
        for k in range(count)
    ]

    barrier = pltpu.get_barrier_semaphore()
    greeted = [-side, 2 * side, -2 * side] + ([] if relay else [side])
    for steps in greeted:
        pl.semaphore_signal(
            barrier, inc=1, device_id={"panel": panel(steps)},
            device_id_type=pl.DeviceIdType.MESH,
        )
    for ahead in range(1, lags):
        pl.semaphore_signal(
            barrier, inc=1, device_id={"lag": lax.rem(lag + ahead, lags)},
            device_id_type=pl.DeviceIdType.MESH,
        )
    pl.semaphore_wait(barrier, len(greeted) + lags - 1)
    local.wait()

    def send(source, slot, block, steps):
        return pltpu.make_async_remote_copy(
            src_ref=source.at[block],
            dst_ref=window.at[slot, block],
            send_sem=send_sem.at[slot - 1, block],
            recv_sem=recv_sem.at[slot - 1, block],
            device_id={"panel": panel(steps)},
            device_id_type=pl.DeviceIdType.MESH,
        )

    first, second, partner, passed = [], [], [], []
    for block in range(blocks):
        first.append(send(outgoing(2 * side), 3, block, 2 * side))
        partner.append(send(outgoing(-side), 4, block, -side))
        first[-1].start()
        partner[-1].start()
    for block in range(blocks):
        second.append(send(outgoing(-2 * side), 2, block, -2 * side))
        second[-1].start()
    near_copy = pltpu.make_async_copy(near_ref, near, near_sem)
    incident_copy = pltpu.make_async_copy(incident_ref, incident, incident_sem)
    for copy in weight_copies:
        copy.start()
    incident_copy.start()
    near_copy.start()
    for block in range(blocks):
        if relay:
            first[block].wait_recv()
            passed.append(send(window.at[3], 1, block, -side))
        else:
            passed.append(send(outgoing(side), 1, block, side))
        passed[-1].start()
    for copy in weight_copies:
        copy.wait()
    incident_copy.wait()
    near_copy.wait()
    for block in range(blocks):
        if not relay:
            first[block].wait_recv()
        partner[block].wait_recv()
        second[block].wait_recv()
        passed[block].wait_recv()

    live = counts_ref[0, 0]
    readers = right.shape[1] // fields
    for k in range(count):
        offset = pairs_ref[0, 0, 0, k]
        slot = pairs_ref[0, 1, 0, k]
        reader = pairs_ref[0, 2, 0, k]
        if relay:
            block = send_ref[0, offset, slot, panel(offset - reach)]
        else:
            block = slot
        place = lax.rem((offset - reach) * side + offsets, offsets)
        value = window[place, block]
        for r in range(readers):
            kept = jnp.logical_and(reader == r, k < live)
            right[k * depth:(k + 1) * depth, r * fields:(r + 1) * fields] = jnp.where(
                kept, value, jnp.zeros_like(value)
            )

    rows = depth // CHUNKS
    sums = []
    for chunk in range(CHUNKS):
        at = slice(chunk * rows, (chunk + 1) * rows)
        total = None
        for k in range(count):
            term = jnp.dot(
                weights[k, at, :], right[k * depth:(k + 1) * depth, :],
                preferred_element_type=jnp.float32,
            )
            total = term if total is None else total + term
        for r in range(readers):
            partial_value[r, at, :] = total[:, r * fields:(r + 1) * fields]
        for ahead in range(1, lags):
            other = lax.rem(lag + ahead, lags)
            copy = pltpu.make_async_remote_copy(
                src_ref=partial_value.at[pl.ds(other * own, own), pl.ds(chunk * rows, rows)],
                dst_ref=landed.at[ahead - 1, :, pl.ds(chunk * rows, rows)],
                send_sem=sum_send_sem.at[ahead - 1, chunk],
                recv_sem=sum_recv_sem.at[ahead - 1, chunk],
                device_id={"lag": other},
                device_id_type=pl.DeviceIdType.MESH,
            )
            copy.start()
            sums.append(copy)
    for copy in first + partner + second + passed:
        copy.wait_send()
    for copy in sums:
        copy.wait_recv()
    for j in range(own):
        summed = partial_value[lag * own + j]
        for ahead in range(1, lags):
            summed = summed + landed[ahead - 1, j]
        remainder = (incident[j].astype(jnp.float32) - summed).astype(jnp.bfloat16)
        out_ref[j] = jnp.dot(
            near[j], remainder, preferred_element_type=jnp.float32
        ).astype(out_ref.dtype)
    for copy in sums:
        copy.wait_send()


def on_device(panels, lags, history, weights, pairs, counts, send_list, incident, near_inverse):
    readers, depth, fields = history.shape[1:]
    offsets, slots = send_list.shape[2:]
    assert offsets == 5 and panels % 2 == 0 and panels > offsets
    count = weights.shape[2]
    own = incident.shape[0]
    relay = readers <= slots
    blocks = readers if relay else slots
    local = history
    if not relay:
        here = lax.axis_index("panel")
        mine = lax.dynamic_index_in_dim(send_list, here, 0, keepdims=False)[0]
        local = jnp.take(history[0], mine.reshape(-1), axis=0).reshape(
            (offsets, slots, depth, fields)
        )
    anywhere = pl.BlockSpec(memory_space=pl.ANY)
    scalars = pl.BlockSpec(memory_space=pltpu.SMEM)
    dma = pltpu.SemaphoreType.DMA
    return pl.pallas_call(
        functools.partial(step_kernel, relay, panels, lags),
        out_shape=jax.ShapeDtypeStruct(incident.shape, jnp.bfloat16),
        in_specs=[scalars] * 3 + [anywhere] * 4,
        out_specs=pl.BlockSpec(memory_space=pltpu.VMEM),
        scratch_shapes=[
            pltpu.VMEM((offsets, blocks, depth, fields), history.dtype),
            pltpu.VMEM(weights.shape[2:], weights.dtype),
            pltpu.VMEM(near_inverse.shape, near_inverse.dtype),
            pltpu.VMEM(incident.shape, incident.dtype),
            pltpu.VMEM((count * depth, readers * fields), history.dtype),
            pltpu.VMEM((readers, depth, fields), jnp.float32),
            pltpu.VMEM((lags - 1, own, depth, fields), jnp.float32),
            dma((offsets - 1, blocks)),
            dma((offsets - 1, blocks)),
            dma,
            dma((count,)),
            dma,
            dma,
            dma((lags - 1, CHUNKS)),
            dma((lags - 1, CHUNKS)),
        ],
        compiler_params=pltpu.CompilerParams(
            collective_id=0, has_side_effects=True, vmem_limit_bytes=67043328
        ),
    )(jnp.transpose(pairs, (0, 3, 1, 2)), counts, jnp.transpose(send_list, (1, 2, 3, 0)), local, weights, incident, near_inverse)


def solution(mesh):
    return jax.shard_map(
        functools.partial(on_device, mesh.shape["panel"], mesh.shape["lag"]),
        mesh=mesh,
        in_specs=(
            P("lag", "panel", None, None),
            P("panel", "lag", None, None, None),
            P("panel", "lag", None, None),
            P("panel", "lag"),
            P(None, "lag", None, None),
            P(("panel", "lag"), None, None),
            P(("panel", "lag"), None, None),
        ),
        out_specs=P(("panel", "lag"), None, None),
        check_vma=False,
    )
```

profile of v0, /device:TPU:5, one launch (start us, length us, event | category | flops | bytes accessed | tf_op | source)
XLA Modules:
  0.0 27.5 jit_solution(3189899486138081150)
XLA Ops:
  0.7 25.3 %shard_map.73 = bf16[1,512,128]{2,1,0:T(8,128)(2,1)} custom-call(s32[1,3,1,6]{3,2,1,0:T(1,128)} %bitcast.3, s32[1,1]{1,0:T(1,128)S(6)} %copy.9.counts_ref, s32[1,5,2,16]{3,2,1,0:T(2,128)} %bitcast.2, bf16[1,2,512,128]{3,2,1,0:T(8,128)(2,1)} %local_ref.1, bf16[1,1,6,512,512]{4,3,2,1,0:T(8,128)(2,1)} %weights_ref.1, bf16[1,512,128]{2,1,0:T(8,128)(2,1)} %incident_ref.1, ...), custom_call_target="tpu_custom_call" | custom-call | tf_op jit(solution)/shard_map/pallas_call | solution.py:179
  26.0 1.6 %copy.10 = bf16[1,512,128]{2,1,0:T(8,128)(2,1)} copy(bf16[1,512,128]{2,1,0:T(8,128)(2,1)} %shard_map.73) | data formatting | bytes 262144
where the time goes:
time: 27.7 us; the launch traced here: 27.5 us
  Pallas kernels  25.3 us (91%)
  local copies, waits for them, and re-layouts  1.57 us (6%)
  between operations  0.66 us (2%)
    pallas_call x1, Pallas kernels, on_device(): pl.pallas_call(functools.partial(step_kernel, relay, panels, lags), out_s...  25.3 us
    unnamed x1, local copies, waits for them, and re-layouts  1.57 us

commit v1 on v0

--- a/solution.py
+++ b/solution.py
@@ -8,13 +8,14 @@
 from jax.sharding import PartitionSpec as P
 
 CHUNKS = 2
+PARTS = 4
 
 
 def step_kernel(
     relay, panels, lags,
     pairs_ref, counts_ref, send_ref, local_ref, weights_ref, incident_ref, near_ref,
     out_ref,
-    window, weights, near, incident, right, partial_value, landed,
+    windows, weights, near, incident, right, running, partial_value, landed,
     send_sem, recv_sem, local_sem, weight_sem, near_sem, incident_sem,
     sum_send_sem, sum_recv_sem,
 ):
@@ -22,7 +23,8 @@
     lag = lax.axis_index("lag")
     offsets = send_ref.shape[1]
     reach = offsets // 2
-    blocks, depth, fields = window.shape[1:]
+    blocks, piece, fields = windows[0].shape[1:]
+    depth = piece * PARTS
     count = weights.shape[0]
     own = incident.shape[0]
     side = 2 * lax.rem(here, 2) - 1
@@ -30,12 +32,23 @@
     def panel(steps):
         return lax.rem(here + steps + panels, panels)
 
-    def outgoing(steps):
-        return local_ref.at[reach - steps] if not relay else window.at[0]
+    def rows_of(part):
+        return pl.ds(part * piece, piece)
+
+    def outgoing(steps, part):
+        if relay:
+            return windows[part].at[0]
+        return local_ref.at[reach - steps, :, rows_of(part)]
 
     source_here = local_ref.at[0] if relay else local_ref.at[reach]
-    local = pltpu.make_async_copy(source_here, window.at[0], local_sem)
-    local.start()
+    locals_here = [
+        pltpu.make_async_copy(
+            source_here.at[:, rows_of(part)], windows[part].at[0], local_sem.at[part]
+        )
+        for part in range(PARTS)
+    ]
+    for copy in locals_here:
+        copy.start()
     weight_copies = [
         pltpu.make_async_copy(weights_ref.at[0, 0, k], weights.at[k], weight_sem.at[k])
         for k in range(count)
@@ -54,53 +67,53 @@
             device_id_type=pl.DeviceIdType.MESH,
         )
     pl.semaphore_wait(barrier, len(greeted) + lags - 1)
-    local.wait()
-
-    def send(source, slot, block, steps):
-        return pltpu.make_async_remote_copy(
-            src_ref=source.at[block],
-            dst_ref=window.at[slot, block],
-            send_sem=send_sem.at[slot - 1, block],
-            recv_sem=recv_sem.at[slot - 1, block],
+    for copy in locals_here:
+        copy.wait()
+
+    def send(source, slot, part, steps):
+        copy = pltpu.make_async_remote_copy(
+            src_ref=source,
+            dst_ref=windows[part].at[slot],
+            send_sem=send_sem.at[slot - 1, part],
+            recv_sem=recv_sem.at[slot - 1, part],
             device_id={"panel": panel(steps)},
             device_id_type=pl.DeviceIdType.MESH,
         )
+        copy.start()
+        return copy
 
     first, second, partner, passed = [], [], [], []
-    for block in range(blocks):
-        first.append(send(outgoing(2 * side), 3, block, 2 * side))
-        partner.append(send(outgoing(-side), 4, block, -side))
-        first[-1].start()
-        partner[-1].start()
-    for block in range(blocks):
-        second.append(send(outgoing(-2 * side), 2, block, -2 * side))
-        second[-1].start()
+    lead = PARTS // 2
+    for step in range(PARTS + lead):
+        if step < PARTS:
+            first.append(send(outgoing(2 * side, step), 3, step, 2 * side))
+            partner.append(send(outgoing(-side, step), 4, step, -side))
+        if step >= lead:
+            part = step - lead
+            second.append(send(outgoing(-2 * side, part), 2, part, -2 * side))
     near_copy = pltpu.make_async_copy(near_ref, near, near_sem)
     incident_copy = pltpu.make_async_copy(incident_ref, incident, incident_sem)
     for copy in weight_copies:
         copy.start()
     incident_copy.start()
     near_copy.start()
-    for block in range(blocks):
+    def pass_on(part):
         if relay:
-            first[block].wait_recv()
-            passed.append(send(window.at[3], 1, block, -side))
+            first[part].wait_recv()
+            passed.append(send(windows[part].at[3], 1, part, -side))
         else:
-            passed.append(send(outgoing(side), 1, block, side))
-        passed[-1].start()
+            passed.append(send(outgoing(side, part), 1, part, side))
+
+    for part in range(PARTS):
+        pass_on(part)
     for copy in weight_copies:
         copy.wait()
     incident_copy.wait()
     near_copy.wait()
-    for block in range(blocks):
-        if not relay:
-            first[block].wait_recv()
-        partner[block].wait_recv()
-        second[block].wait_recv()
-        passed[block].wait_recv()
 
     live = counts_ref[0, 0]
-    readers = right.shape[1] // fields
+    readers = right.shape[2] // fields
+    chosen = []
     for k in range(count):
         offset = pairs_ref[0, 0, 0, k]
         slot = pairs_ref[0, 1, 0, k]
@@ -110,24 +123,40 @@
         else:
             block = slot
         place = lax.rem((offset - reach) * side + offsets, offsets)
-        value = window[place, block]
-        for r in range(readers):
-            kept = jnp.logical_and(reader == r, k < live)
-            right[k * depth:(k + 1) * depth, r * fields:(r + 1) * fields] = jnp.where(
-                kept, value, jnp.zeros_like(value)
-            )
+        chosen.append((place, block, reader))
+
+    def arrive(part):
+        if not relay:
+            first[part].wait_recv()
+        partner[part].wait_recv()
+        second[part].wait_recv()
+        passed[part].wait_recv()
+        for k, (place, block, reader) in enumerate(chosen):
+            value = windows[part][place, block]
+            for r in range(readers):
+                kept = jnp.logical_and(reader == r, k < live)
+                right[part, k * piece:(k + 1) * piece, r * fields:(r + 1) * fields] = jnp.where(
+                    kept, value, jnp.zeros_like(value)
+                )
+
+    def product(part, at):
+        left = jnp.concatenate(
+            [weights[k, at, part * piece:(part + 1) * piece] for k in range(count)], axis=1
+        )
+        return jnp.dot(left, right[part], preferred_element_type=jnp.float32)
 
     rows = depth // CHUNKS
     sums = []
+    for part in range(PARTS - 1):
+        arrive(part)
+        for chunk in range(CHUNKS):
+            at = slice(chunk * rows, (chunk + 1) * rows)
+            term = product(part, at)
+            running[at, :] = term if part == 0 else running[at, :] + term
+    arrive(PARTS - 1)
     for chunk in range(CHUNKS):
         at = slice(chunk * rows, (chunk + 1) * rows)
-        total = None
-        for k in range(count):
-            term = jnp.dot(
-                weights[k, at, :], right[k * depth:(k + 1) * depth, :],
-                preferred_element_type=jnp.float32,
-            )
-            total = term if total is None else total + term
+        total = running[at, :] + product(PARTS - 1, at)
         for r in range(readers):
             partial_value[r, at, :] = total[:, r * fields:(r + 1) * fields]
         for ahead in range(1, lags):
@@ -182,16 +211,17 @@
         in_specs=[scalars] * 3 + [anywhere] * 4,
         out_specs=pl.BlockSpec(memory_space=pltpu.VMEM),
         scratch_shapes=[
-            pltpu.VMEM((offsets, blocks, depth, fields), history.dtype),
+            [pltpu.VMEM((offsets, blocks, depth // PARTS, fields), history.dtype)] * PARTS,
             pltpu.VMEM(weights.shape[2:], weights.dtype),
             pltpu.VMEM(near_inverse.shape, near_inverse.dtype),
             pltpu.VMEM(incident.shape, incident.dtype),
-            pltpu.VMEM((count * depth, readers * fields), history.dtype),
+            pltpu.VMEM((PARTS, count * depth // PARTS, readers * fields), history.dtype),
+            pltpu.VMEM((depth, readers * fields), jnp.float32),
             pltpu.VMEM((readers, depth, fields), jnp.float32),
             pltpu.VMEM((lags - 1, own, depth, fields), jnp.float32),
-            dma((offsets - 1, blocks)),
-            dma((offsets - 1, blocks)),
-            dma,
+            dma((offsets - 1, PARTS)),
+            dma((offsets - 1, PARTS)),
+            dma((PARTS,)),
             dma((count,)),
             dma,
             dma,

time: 27.7 us -> 25.3 us (0.913)
  Pallas kernels: 25.3 us -> 22.9 us
    pallas_call x1, Pallas kernels: 25.3 us -> 22.9 us  [on_device(): pl.pallas_call(functools.partial(step_kernel, relay, panels, lags), out_s...]
where the time goes in v1:
time: 25.3 us; the launch traced here: 25.1 us
  Pallas kernels  22.9 us (91%)
  local copies, waits for them, and re-layouts  1.57 us (6%)
  between operations  0.66 us (3%)
    pallas_call x1, Pallas kernels, on_device(): pl.pallas_call(functools.partial(step_kernel, relay, panels, lags), out_s...  22.9 us
    unnamed x1, local copies, waits for them, and re-layouts  1.57 us

profile of v1, /device:TPU:5, one launch (start us, length us, event | category | flops | bytes accessed | tf_op | source)
XLA Modules:
  0.0 25.1 jit_solution(16846245785064019495)
XLA Ops:
  0.7 22.9 %shard_map.73 = bf16[1,512,128]{2,1,0:T(8,128)(2,1)} custom-call(s32[1,3,1,6]{3,2,1,0:T(1,128)} %bitcast.3, s32[1,1]{1,0:T(1,128)S(6)} %copy.9.counts_ref, s32[1,5,2,16]{3,2,1,0:T(2,128)} %bitcast.2, bf16[1,2,512,128]{3,2,1,0:T(8,128)(2,1)} %local_ref.1, bf16[1,1,6,512,512]{4,3,2,1,0:T(8,128)(2,1)} %weights_ref.1, bf16[1,512,128]{2,1,0:T(8,128)(2,1)} %incident_ref.1, ...), custom_call_target="tpu_custom_call" | custom-call | tf_op jit(solution)/shard_map/pallas_call | solution.py:208
  23.6 1.6 %copy.10 = bf16[1,512,128]{2,1,0:T(8,128)(2,1)} copy(bf16[1,512,128]{2,1,0:T(8,128)(2,1)} %shard_map.73) | data formatting | bytes 262144
